TPU v7x, 32 devices: a whole 2x2x4 slice. The times are simulated.
32 devices in a mesh: seq: 8 (over z, x), head: 4 (over y, core).
Axes of the slice: x: 2, y: 2, z: 4, core: 2. Of those that a mesh axis runs over, the one named last changes fastest.
Arguments:
- queries: bfloat16 [8192, 2048], P('seq', 'head'), may hold values from -64 to 64
- keys: bfloat16 [8192, 2048], P('seq', 'head'), may hold values from -16 to 16
- values: bfloat16 [8192, 2048], P('seq', 'head'), may hold values from -6 to 6
- span_bounds: int32 [16, 2], replicated, may hold values from 0 to 8192, as said below
- mem_decay: float32 [8, 16], P(None, 'head'), may hold values from 0.01 to 1
- mem_gate: float32 [16], P('head'), may hold values from -2 to 2
- out_weight: bfloat16 [2048, 4096], P('head'), may hold values from -0.125 to 0.125
Outputs:
- mixed: bfloat16 [8192, 4096], P('seq', 'head')
Inputs may be any that keep to these rules, and one draw needn't show every extreme that they name: `span_bounds`: slot k lies in segment k // 2, inside the k % 2-th of 2 equal parts of it; start <= end, an empty slot has start == end; some slot covers a whole part.
All inputs are finite; a program needn't handle non-finite values.
Results may differ from a plain program's by a relative error of at most 0.0052.
The roundings to bfloat16 on the way count: a program that leaves them out, or rounds other values in their place, can miss the bound.
Values may be sent and summed in bfloat16 or wider, within the bound.
No kernel may reach another device: no remote copies, remote signals or barrier semaphores. Data moves between devices by JAX's collectives and lax.ppermute only.
A program may use at most 128 MiB of HBM per device.

v0:
```python
import math
import jax
import jax.numpy as jnp
from jax import lax
from jax.sharding import PartitionSpec as P

BAND = 512
SPAN_DEV = 2
HIGHEST_PRECISION = lax.Precision.HIGHEST


def from_behind(block, axis, distance):
    devices = range(lax.axis_size(axis))
    route = [(i - distance, i) for i in devices if i - distance in devices]
    return lax.ppermute(block, axis, route)


def feature_map(values_in):
    return jnp.where(values_in > 0, values_in + 1.0, jnp.exp(jnp.minimum(values_in, 0.0)))


def local_attention(
    queries_3d, band_keys, band_values, query_labels, key_labels, shard_index, band_width
):
    seg_rows, head_count, head_width = queries_3d.shape
    block_rows = min(seg_rows, 512)
    key_count = band_keys.shape[0]
    key_pos = jnp.arange(key_count) - band_width
    key_valid = (key_pos >= 0) | (shard_index > 0)
    score_scale = 1.0 / math.sqrt(head_width)

    def attend_block(block_index):
        row_start = block_index * block_rows
        query_block = lax.dynamic_slice_in_dim(queries_3d, row_start, block_rows, 0)
        label_block = lax.dynamic_slice_in_dim(query_labels, row_start, block_rows, 0)
        query_pos = row_start + jnp.arange(block_rows)
        scores = (
            jnp.einsum("qhd,khd->hqk", query_block, band_keys, preferred_element_type=jnp.float32)
            * score_scale
        )
        nearby = (
            (key_pos[None, :] <= query_pos[:, None])
            & (key_pos[None, :] > query_pos[:, None] - band_width)
            & key_valid[None, :]
        )
        same_span = (label_block[:, None] > 0) & (label_block[:, None] == key_labels[None, :])
        visible = nearby | same_span
        scores = jnp.where(visible[None], scores, -1e30)
        top_score = jnp.max(scores, axis=-1, keepdims=True)
        weights = jnp.exp(scores - top_score)
        totals = jnp.sum(weights, axis=-1)
        mixed_out = jnp.einsum(
            "hqk,khd->qhd",
            weights.astype(jnp.bfloat16),
            band_values,
            preferred_element_type=jnp.float32,
        )
        return mixed_out / jnp.transpose(totals)[:, :, None]

    blocks = lax.map(attend_block, jnp.arange(seg_rows // block_rows))
    return blocks.reshape(seg_rows, head_count, head_width)


def body(queries, keys, values, span_bounds, mem_decay, mem_gate, out_weight):
    seg_rows = queries.shape[0]
    head_count = mem_gate.shape[0]
    head_width = queries.shape[1] // head_count
    band_width = BAND
    shard_index = lax.axis_index("seq")
    prev_keys, prev_values = from_behind(
        (keys[seg_rows - band_width :], values[seg_rows - band_width :]), "seq", 1
    )
    key_feats = feature_map(keys.astype(jnp.float32)).reshape(seg_rows, head_count, head_width)
    value_rows = values.astype(jnp.float32).reshape(seg_rows, head_count, head_width)
    state = jnp.einsum("thd,the->hde", key_feats, value_rows, precision=HIGHEST_PRECISION)
    feat_sum = jnp.sum(key_feats, axis=0)
    cumulative = jnp.cumsum(jnp.log(mem_decay), axis=0)
    before = lax.dynamic_index_in_dim(
        cumulative, jnp.maximum(shard_index - 1, 0), 0, keepdims=False
    )
    part_state = lax.all_gather(state[None], "seq", axis=0, tiled=True)
    part_sum = lax.all_gather(feat_sum[None], "seq", axis=0, tiled=True)
    piece_count = part_state.shape[0]
    piece_index = jnp.arange(piece_count)
    factor = jnp.where(
        (piece_index < shard_index)[:, None],
        jnp.exp(jnp.minimum(before[None, :] - cumulative, 0.0)),
        0.0,
    )
    memory = jnp.einsum("nh,nhde->hde", factor, part_state, precision=HIGHEST_PRECISION)
    feat_total = jnp.einsum("nh,nhd->hd", factor, part_sum, precision=HIGHEST_PRECISION)
    query_feats = feature_map(queries.astype(jnp.float32)).reshape(seg_rows, head_count, head_width)
    numer = jnp.einsum("thd,hde->the", query_feats, memory, precision=HIGHEST_PRECISION)
    denom = jnp.einsum("thd,hd->th", query_feats, feat_total, precision=HIGHEST_PRECISION) + 1.0
    readout = numer / denom[:, :, None]
    own_spans = lax.dynamic_slice_in_dim(span_bounds, shard_index * SPAN_DEV, SPAN_DEV, 0)
    positions = shard_index * seg_rows + jnp.arange(seg_rows)
    inside = (positions[:, None] >= own_spans[None, :, 0]) & (
        positions[:, None] < own_spans[None, :, 1]
    )
    slot_ids = (jnp.arange(SPAN_DEV) + 1)[None, :]
    query_labels = jnp.sum(inside.astype(jnp.int32) * slot_ids, axis=1)
    key_labels = jnp.concatenate([jnp.zeros((band_width,), jnp.int32), query_labels])
    band_keys = jnp.concatenate([prev_keys, keys], axis=0).reshape(
        band_width + seg_rows, head_count, head_width
    )
    band_values = jnp.concatenate([prev_values, values], axis=0).reshape(
        band_width + seg_rows, head_count, head_width
    )
    queries_3d = queries.reshape(seg_rows, head_count, head_width)
    local = local_attention(
        queries_3d, band_keys, band_values, query_labels, key_labels, shard_index, band_width
    )
    gate = jax.nn.sigmoid(mem_gate)[None, :, None]
    attended = (
        (gate * readout + (1.0 - gate) * local)
        .astype(jnp.bfloat16)
        .reshape(seg_rows, head_count * head_width)
    )
    gathered = lax.all_gather(attended, "head", axis=1, tiled=True)
    columns = lax.all_to_all(out_weight, "head", split_axis=1, concat_axis=0, tiled=True)
    mixed = jnp.dot(gathered, columns, preferred_element_type=jnp.float32)
    return mixed.astype(jnp.bfloat16)


def solution(mesh):
    return jax.shard_map(
        body,
        mesh=mesh,
        in_specs=(
            P("seq", "head"),
            P("seq", "head"),
            P("seq", "head"),
            P(),
            P(None, "head"),
            P("head"),
            P("head", None),
        ),
        out_specs=P("seq", "head"),
        check_vma=False,
    )
```

profile of v0, /device:TPU:0, one launch (start us, length us, event | category | flops | bytes accessed | tf_op | source)
XLA Modules:
  0.0 270.6 jit_solution(7278276117064473592)
XLA Ops:
  6.5 1.6 copy.56
  9.0 5.7 %collective-permute-start = (bf16[512,512]{0,1:T(8,128)(2,1)}, bf16[512,512]{0,1:T(8,128)(2,1)}, u32[]{:S(2)}, u32[]{:S(2)}) collective-permute-start(bf16[512,512]{0,1:T(8,128)(2,1)} %slice.16), channel_id=1, source_target_pairs={{0,4},{4,8},{8,12},{12,16},{16,20},{20,24},{24,28},{1,5},{5,9},{9,... | collective-permute-start | bytes 1572872 | tf_op jit(solution)/shard_map/ppermute | solution.py:15
  16.1 3.5 %collective-permute-start.1 = (bf16[512,512]{0,1:T(8,128)(2,1)}, bf16[512,512]{0,1:T(8,128)(2,1)}, u32[]{:S(2)}, u32[]{:S(2)}) collective-permute-start(bf16[512,512]{0,1:T(8,128)(2,1)} %slice.17), channel_id=1, source_target_pairs={{0,4},{4,8},{8,12},{12,16},{16,20},{20,24},{24,28},{1,5},{5,9},{9,... | collective-permute-start | bytes 1572872 | tf_op jit(solution)/shard_map/ppermute | solution.py:15
  19.6 1.8 fusion.35
  21.4 1.8 copy.75
  23.2 3.8 %fusion.29 = f32[4,128,128]{2,1,0:T(8,128)} fusion(f32[1024,4,128]{0,2,1:T(8,128)} %bitcast.87, bf16[1024,512]{1,0:T(8,128)(2,1)} %param.11), kind=kOutput, calls=%fused_computation.42 | convolution fusion | flops 805306368 | bytes 3407872 | tf_op jit(solution)/shard_map/thd,the->hde/dot_general | solution.py:75
  27.1 37.5 %all_gather.10 = f32[8,4,128]{2,1,0:T(4,128)S(1)} all-gather(f32[1,4,128]{2,1,0:T(4,128)S(1)} %bitcast.97), channel_id=1, replica_groups=mesh['seq'=8,'head'=4] {'seq'}, dimensions={0}, use_global_device_ids=true | all-gather | bytes 18432 | tf_op jit(solution)/shard_map/all_gather | solution.py:82
  64.7 1.8 fusion.22
  66.5 1.9 copy.81
  70.3 2.3 copy.55
  72.6 2.6 pad_maximum_fusion
  75.2 1.9 copy.61
  77.2 2.3 pad_maximum_fusion.1
  79.5 2.6 copy.62
  82.1 77.2 %while.14 = (s32[]{:T(128)}, f32[2,512,4,128]{1,0,3,2:T(2,128)}, s32[2]{0:T(128)S(1)}, s32[1024]{0:T(1024)S(1)}, s32[1536]{0:T(1024)S(1)}, /*index=5*/bf16[1024,...) while((s32[]{:T(128)}, f32[2,512,4,128]{1,0,3,2:T(2,128)}, ...), condition=%wide.region_6.7_spmd.clone.clone, body=%wide.region_3.6_spmd.clone.clone.sunk | while | flops 1650986496 | bytes 49885384 | solution.py:60
  84.9 4.1 %fusion.57 = (f32[4,512]{1,0:T(4,128)S(1)}, f32[4,512,1536]{2,1,0:T(8,128)S(1)}) fusion(pred[512,1536]{1,0:T(8,128)(4,1)S(1)} %and_or_fusion.2, bf16[1536,4,128]{2,0,1:T(8,128)(2,1)S(1)} %get-tuple-element.345, bf16[1024,4,128]{0,2,1:T(8,128)(2,1)} %get-tuple-element.344, s32[]{:T(128)S(6)} %select_n.64), kind=kOutput, calls=%fused_computation.4.clone.1 | convolution fusion | flops 814741504 | bytes 15474692 | tf_op jit(solution)/shard_map/while/body/eval_jaxpr/qhd,khd->hqk/dot_general | solution.py:38
  89.0 3.6 %fusion.58 = f32[4,512]{1,0:T(4,128)S(1)} fusion(f32[4,512,1536]{2,1,0:T(8,128)S(1)} %get-tuple-element.311, f32[4,512]{1,0:T(4,128)S(1)} %get-tuple-element.312, pred[512,1536]{1,0:T(8,128)(4,1)S(1)} %and_or_fusion.2), kind=kLoop, calls=%fused_computation.5.clone.1 | loop fusion | flops 12580864 | bytes 13385728 | tf_op jit(solution)/shard_map/while/body/eval_jaxpr/reduce_sum | solution.py:51
  92.7 6.0 %divide_bitcast_fusion.2 = f32[1,512,4,128]{3,1,2,0:T(8,128)} fusion(bf16[1536,4,128]{2,0,1:T(8,128)(2,1)} %get-tuple-element.346, f32[4,512,1536]{2,1,0:T(8,128)S(1)} %get-tuple-element.311, f32[4,512]{1,0:T(4,128)S(1)} %get-tuple-element.312, pred[512,1536]{1,0:T(8,128)(4,1)S(1)} %and_or_fusion.2, f32[512,4]{0,1:T(4,128)S(1)} %bitcast.94), kind=kOutput, calls=%fused_computation.11.clone.1 | convolution fusion | flops 818151424 | bytes 16007168 | tf_op jit(solution)/shard_map/while/body/eval_jaxpr/hqk,khd->qhd/dot_general | solution.py:52
  98.7 2.4 copy.93
  101.1 19.6 %dynamic_update_slice.10 = f32[2,512,4,128]{1,0,3,2:T(2,128)} dynamic-update-slice(f32[2,512,4,128]{1,0,3,2:T(2,128)} %get-tuple-element.327, f32[1,512,4,128]{1,0,3,2:T(1,128)S(1)} %copy.93, s32[]{:T(128)} %get-tuple-element.326, s32[]{:T(128)} %constant.90.clone.1..sunk, s32[]{:T(128)} %constant.90.clone.1..sunk, s32[]{:T(128)} %constant.90.clone.1..sunk) | dynamic-update-slice | bytes 2097156 | tf_op jit(solution)/shard_map/while/body/jit(dynamic_update_index_in_dim)/dynamic_update_slice | solution.py:60
  123.5 4.1 %fusion.57 = (f32[4,512]{1,0:T(4,128)S(1)}, f32[4,512,1536]{2,1,0:T(8,128)S(1)}) fusion(pred[512,1536]{1,0:T(8,128)(4,1)S(1)} %and_or_fusion.2, bf16[1536,4,128]{2,0,1:T(8,128)(2,1)S(1)} %get-tuple-element.345, bf16[1024,4,128]{0,2,1:T(8,128)(2,1)} %get-tuple-element.344, s32[]{:T(128)S(6)} %select_n.64), kind=kOutput, calls=%fused_computation.4.clone.1 | convolution fusion | flops 814741504 | bytes 15474692 | tf_op jit(solution)/shard_map/while/body/eval_jaxpr/qhd,khd->hqk/dot_general | solution.py:38
  127.6 3.6 %fusion.58 = f32[4,512]{1,0:T(4,128)S(1)} fusion(f32[4,512,1536]{2,1,0:T(8,128)S(1)} %get-tuple-element.311, f32[4,512]{1,0:T(4,128)S(1)} %get-tuple-element.312, pred[512,1536]{1,0:T(8,128)(4,1)S(1)} %and_or_fusion.2), kind=kLoop, calls=%fused_computation.5.clone.1 | loop fusion | flops 12580864 | bytes 13385728 | tf_op jit(solution)/shard_map/while/body/eval_jaxpr/reduce_sum | solution.py:51
  131.3 6.0 %divide_bitcast_fusion.2 = f32[1,512,4,128]{3,1,2,0:T(8,128)} fusion(bf16[1536,4,128]{2,0,1:T(8,128)(2,1)} %get-tuple-element.346, f32[4,512,1536]{2,1,0:T(8,128)S(1)} %get-tuple-element.311, f32[4,512]{1,0:T(4,128)S(1)} %get-tuple-element.312, pred[512,1536]{1,0:T(8,128)(4,1)S(1)} %and_or_fusion.2, f32[512,4]{0,1:T(4,128)S(1)} %bitcast.94), kind=kOutput, calls=%fused_computation.11.clone.1 | convolution fusion | flops 818151424 | bytes 16007168 | tf_op jit(solution)/shard_map/while/body/eval_jaxpr/hqk,khd->qhd/dot_general | solution.py:52
  137.3 2.4 copy.93
  139.7 19.6 %dynamic_update_slice.10 = f32[2,512,4,128]{1,0,3,2:T(2,128)} dynamic-update-slice(f32[2,512,4,128]{1,0,3,2:T(2,128)} %get-tuple-element.327, f32[1,512,4,128]{1,0,3,2:T(1,128)S(1)} %copy.93, s32[]{:T(128)} %get-tuple-element.326, s32[]{:T(128)} %constant.90.clone.1..sunk, s32[]{:T(128)} %constant.90.clone.1..sunk, s32[]{:T(128)} %constant.90.clone.1..sunk) | dynamic-update-slice | bytes 2097156 | tf_op jit(solution)/shard_map/while/body/jit(dynamic_update_index_in_dim)/dynamic_update_slice | solution.py:60
  159.3 4.0 %reshape.179 = f32[1024,4,128]{0,2,1:T(8,128)} reshape(f32[2,512,4,128]{1,0,3,2:T(2,128)} %get-tuple-element.133) | data formatting | bytes 4194304 | tf_op jit(solution)/shard_map/reshape | solution.py:61
  163.3 4.6 %fusion.27 = f32[4,1,128,128]{3,1,2,0:T(1,128)S(1)} fusion(f32[8,4,1,1]{0,2,3,1:T(1,128)S(1)} %bitcast.96, f32[8,4,128,128]{3,2,1,0:T(8,128)} %bitcast.91), kind=kOutput, calls=%fused_computation.36 | convolution fusion | flops 6291456 | bytes 2359424 | tf_op jit(solution)/shard_map/nh,nhde->hde/dot_general | solution.py:90
  167.9 4.8 %fusion.26 = bf16[1024,4,128]{0,2,1:T(8,128)(2,1)} fusion(f32[1024,4,128]{0,2,1:T(8,128)} %reshape.179, f32[4,128,128]{2,1,0:T(8,128)S(1)} %bitcast.93, f32[1024,4,128]{0,2,1:T(8,128)S(1)} %bitcast.86, f32[4]{0:T(128)S(1)} %get-tuple-element.236, f32[1024,4]{0,1:T(4,128)S(1)} %fusion.32, f32[4]{0:T(128)S(1)} %get-tuple-element.237), kind=kOutput, calls=%fused_computation.35 | convolution fusion | flops 807927808 | bytes 5521440 | tf_op jit(solution)/shard_map/thd,hde->the/dot_general | solution.py:93
  172.7 6.6 %copy.64 = bf16[512,4096]{0,1:T(8,128)(2,1)} copy(bf16[512,4096]{1,0:T(8,128)(2,1)} %param.15) | data formatting | bytes 8388608 | tf_op args[6]
  179.3 68.7 %all_to_all.19 = bf16[512,4,1024]{0,2,1:T(8,128)(2,1)} all-to-all(bf16[512,4,1024]{0,2,1:T(8,128)(2,1)} %bitcast.84), channel_id=1, replica_groups=mesh['seq'=8,'head'=4] {'head'}, dimensions={1} | all-to-all | bytes 8388608 | tf_op jit(solution)/shard_map/all_to_all | solution.py:121
  248.0 6.3 %copy.65 = bf16[4,512,1024]{2,1,0:T(8,128)(2,1)} copy(bf16[4,512,1024]{1,2,0:T(8,128)(2,1)} %bitcast.83) | data formatting | bytes 8388608 | tf_op jit(solution)/shard_map/all_to_all | solution.py:121
  254.3 9.4 %convolution_convert_fusion = bf16[1024,1024]{1,0:T(8,128)(2,1)} fusion(bf16[1024,2048]{0,1:T(8,128)(2,1)} %all-gather.4.cloned.1.call-done, bf16[2048,1024]{1,0:T(8,128)(2,1)} %bitcast.90), kind=kOutput, calls=%fused_computation.38 | convolution fusion | flops 4296015872 | bytes 10485760 | tf_op jit(solution)/shard_map/dot_general | solution.py:122
  (58 shorter events, 8.6 us)
Async XLA Ops:
  6.5 20.5 %copy-start = (s32[16,2]{0,1:T(2,128)S(1)}, s32[16,2]{0,1:T(2,128)}, u32[]{:S(2)}) copy-start(s32[16,2]{0,1:T(2,128)} %param.12) | copy-start | bytes 388
  6.5 8.2 %copy-start.6 = (bf16[1024,512]{1,0:T(8,128)(2,1)S(1)}, bf16[1024,512]{1,0:T(8,128)(2,1)}, u32[]{:S(2)}) copy-start(bf16[1024,512]{1,0:T(8,128)(2,1)} %param.11) | copy-start | bytes 3145732
  6.5 156.8 %all-gather.6.cloned.1.call-start = ((), (), s32[]{:S(2)}) async-start(), calls=%async_computation.2 | async-start | bytes 2359296 | tf_op jit(solution)/shard_map/all_gather | solution.py:81
  8.1 8.0 %copy-start.4 = (bf16[1024,512]{0,1:T(8,128)(2,1)}, bf16[1024,512]{0,1:T(8,128)(2,1)S(1)}, u32[]{:S(2)}) copy-start(bf16[1024,512]{0,1:T(8,128)(2,1)S(1)} %copy.56) | copy-start | bytes 3145732
  9.0 63.6 %collective-permute-start = (bf16[512,512]{0,1:T(8,128)(2,1)}, bf16[512,512]{0,1:T(8,128)(2,1)}, u32[]{:S(2)}, u32[]{:S(2)}) collective-permute-start(bf16[512,512]{0,1:T(8,128)(2,1)} %slice.16), channel_id=1, source_target_pairs={{0,4},{4,8},{8,12},{12,16},{16,20},{20,24},{24,28},{1,5},{5,9},{9,... | collective-permute-start | bytes 1572872 | tf_op jit(solution)/shard_map/ppermute | solution.py:15
  16.1 61.0 %collective-permute-start.1 = (bf16[512,512]{0,1:T(8,128)(2,1)}, bf16[512,512]{0,1:T(8,128)(2,1)}, u32[]{:S(2)}, u32[]{:S(2)}) collective-permute-start(bf16[512,512]{0,1:T(8,128)(2,1)} %slice.17), channel_id=1, source_target_pairs={{0,4},{4,8},{8,12},{12,16},{16,20},{20,24},{24,28},{1,5},{5,9},{9,... | collective-permute-start | bytes 1572872 | tf_op jit(solution)/shard_map/ppermute | solution.py:15
  23.2 4.0 %copy-start.7 = (f32[8,4]{0,1:T(4,128)S(1)}, f32[8,4]{0,1:T(4,128)}, u32[]{:S(2)}) copy-start(f32[8,4]{0,1:T(4,128)} %param.13) | copy-start | bytes 388
  23.2 41.5 %copy-start.5 = (bf16[1024,512]{1,0:T(8,128)(2,1)S(1)}, bf16[1024,512]{1,0:T(8,128)(2,1)}, u32[]{:S(2)}) copy-start(bf16[1024,512]{1,0:T(8,128)(2,1)} %param.9) | copy-start | bytes 3145732
  27.0 227.4 %all-gather.4.cloned.1.call-start = ((), (), s32[]{:S(2)}) async-start(), calls=%async_computation.1 | async-start | bytes 5242880 | tf_op jit(solution)/shard_map/all_gather | solution.py:120
  68.4 4.2 %copy-start.2 = (f32[1024,512]{0,1:T(8,128)}, f32[1024,512]{0,1:T(8,128)S(1)}, u32[]{:S(2)}) copy-start(f32[1024,512]{0,1:T(8,128)S(1)} %copy.81) | copy-start | bytes 6291460
  68.4 1.7 copy-start.8
  163.3 4.6 %copy-start.3 = (f32[1024,512]{0,1:T(8,128)S(1)}, f32[1024,512]{0,1:T(8,128)}, u32[]{:S(2)}) copy-start(f32[1024,512]{0,1:T(8,128)} %copy-done.2) | copy-start | bytes 6291460
  254.3 9.4 %copy-start.1 = (s32[16,2]{0,1:T(2,128)S(1)}, s32[16,2]{0,1:T(2,128)}, u32[]{:S(2)}) copy-start(s32[16,2]{0,1:T(2,128)} %param.12) | copy-start | bytes 388
Sparse Core Ops, SparseCore 0:
  27.1 49.7 all-gather.5
  172.8 46.6 all-gather.3
where the time goes:
time: 274 us; the launch traced here: 271 us
  blocking collectives  106 us (39%)
  local copies, waits for them, and re-layouts  76.8 us (28%)
  matrix products  44 us (16%)
  other arithmetic  19.3 us (7%)
  between operations  13.6 us (5%)
  starting transfers between devices  9.21 us (3%)
    all_to_all x1, blocking collectives, body(): lax.all_to_all(out_weight, 'head', split_axis=1, concat_axis=0, tiled=True)  68.7 us
    dynamic_update_slice x4, local copies, waits for them, and re-layouts, local_attention(): blocks = lax.map(attend_block, jnp.arange(seg_rows // block_rows))  44 us
    all_gather x1, blocking collectives, body(): part_sum = lax.all_gather(feat_sum[None], 'seq', axis=0, tiled=True)  37.5 us
    unnamed x24, local copies, waits for them, and re-layouts  15.5 us
    dot_general x2, matrix products, attend_block(): jnp.einsum('hqk,khd->qhd', weights.astype(jnp.bfloat16), band_values, pre...  12 us
    dot_general x1, matrix products, body(): mixed = jnp.dot(gathered, columns, preferred_element_type=jnp.float32)  9.37 us
    ppermute x2, starting transfers between devices, from_behind(): return lax.ppermute(block, axis, route)  9.17 us
    dot_general x2, matrix products, attend_block(): jnp.einsum('qhd,khd->hqk', query_block, band_keys, preferred_element_type...  8.27 us
  transfers between devices with their start and end apart: 4, of which 0 were waited for; matrix products, arithmetic and copies ran while one was open for 44% of the time, Pallas kernels for 0%

commit v1 on v0

--- a/solution.py
+++ b/solution.py
@@ -7,6 +7,18 @@
 BAND = 512
 SPAN_DEV = 2
 HIGHEST_PRECISION = lax.Precision.HIGHEST
+
+
+def summed_around(x, axis, dim, product):
+    size, here, extent = (lax.axis_size(axis), lax.axis_index(axis), x.shape[dim])
+    right = [(i, (i + 1) % size) for i in range(size)]
+    held, running = (x, None)
+    for lap in range(size):
+        following = lax.ppermute(held, axis, right) if lap < size - 1 else None
+        absorb = product(held, (here - lap) % size * extent)
+        running = absorb if running is None else running + absorb
+        held = following
+    return running
 
 
 def from_behind(block, axis, distance):
@@ -79,7 +91,6 @@
         cumulative, jnp.maximum(shard_index - 1, 0), 0, keepdims=False
     )
     part_state = lax.all_gather(state[None], "seq", axis=0, tiled=True)
-    part_sum = lax.all_gather(feat_sum[None], "seq", axis=0, tiled=True)
     piece_count = part_state.shape[0]
     piece_index = jnp.arange(piece_count)
     factor = jnp.where(
@@ -88,7 +99,17 @@
         0.0,
     )
     memory = jnp.einsum("nh,nhde->hde", factor, part_state, precision=HIGHEST_PRECISION)
-    feat_total = jnp.einsum("nh,nhd->hd", factor, part_sum, precision=HIGHEST_PRECISION)
+    feat_total = summed_around(
+        feat_sum[None],
+        "seq",
+        0,
+        lambda own_block, start: jnp.einsum(
+            "nh,nhd->hd",
+            lax.dynamic_slice_in_dim(factor, start, own_block.shape[0], axis=0),
+            own_block,
+            precision=HIGHEST_PRECISION,
+        ),
+    )
     query_feats = feature_map(queries.astype(jnp.float32)).reshape(seg_rows, head_count, head_width)
     numer = jnp.einsum("thd,hde->the", query_feats, memory, precision=HIGHEST_PRECISION)
     denom = jnp.einsum("thd,hd->th", query_feats, feat_total, precision=HIGHEST_PRECISION) + 1.0

time: 274 us -> 282 us (1.029)
  waiting for transfers between devices: 0.04 us -> 41.3 us
  blocking collectives: 106 us -> 68.8 us
  starting transfers between devices: 9.21 us -> 12.4 us
    ppermute x0 -> x7, waiting for transfers between devices: none -> 41.3 us  [summed_around(): following = lax.ppermute(held, axis, right) if lap < size - 1 else None]
    all_gather x1 -> x0, blocking collectives: 37.5 us -> none  [body(): part_sum = lax.all_gather(feat_sum[None], 'seq', axis=0, tiled=True)]
    ppermute x0 -> x7, starting transfers between devices: none -> 3.2 us  [summed_around(): following = lax.ppermute(held, axis, right) if lap < size - 1 else None]
    unnamed x24 -> x22, local copies, waits for them, and re-layouts: 15.5 us -> 15.5 us
  transfers between devices with their start and end apart: 4 -> 11, of which waited for: 0 -> 7; matrix products, arithmetic and copies ran while one was open for 44% -> 43% of each run, Pallas kernels for 0% -> 0%
where the time goes in v1:
time: 282 us; the launch traced here: 279 us
  local copies, waits for them, and re-layouts  77 us (27%)
  blocking collectives  68.8 us (24%)
  matrix products  45.5 us (16%)
  waiting for transfers between devices  41.3 us (15%)
  other arithmetic  18.9 us (7%)
  between operations  13.5 us (5%)
  starting transfers between devices  12.4 us (4%)
    all_to_all x1, blocking collectives, body(): lax.all_to_all(out_weight, 'head', split_axis=1, concat_axis=0, tiled=True)  68.8 us
    dynamic_update_slice x4, local copies, waits for them, and re-layouts, local_attention(): blocks = lax.map(attend_block, jnp.arange(seg_rows // block_rows))  44 us
    ppermute x7, waiting for transfers between devices, summed_around(): following = lax.ppermute(held, axis, right) if lap < size - 1 else None  41.3 us
    unnamed x22, local copies, waits for them, and re-layouts  15.5 us
    dot_general x2, matrix products, attend_block(): jnp.einsum('hqk,khd->qhd', weights.astype(jnp.bfloat16), band_values, pre...  12.1 us
    dot_general x1, matrix products, body(): mixed = jnp.dot(gathered, columns, preferred_element_type=jnp.float32)  9.37 us
    ppermute x2, starting transfers between devices, from_behind(): return lax.ppermute(block, axis, route)  9.18 us
    dot_general x2, matrix products, attend_block(): jnp.einsum('qhd,khd->hqk', query_block, band_keys, preferred_element_type...  8.27 us
  transfers between devices with their start and end apart: 11, of which 7 were waited for; matrix products, arithmetic and copies ran while one was open for 43% of the time, Pallas kernels for 0%

profile of v1, /device:TPU:0, one launch (start us, length us, event | category | flops | bytes accessed | tf_op | source)
XLA Modules:
  0.0 278.6 jit_solution(2424444318245024506)
XLA Ops:
  9.0 5.7 %collective-permute-start.7 = (bf16[512,512]{0,1:T(8,128)(2,1)}, bf16[512,512]{0,1:T(8,128)(2,1)}, u32[]{:S(2)}, u32[]{:S(2)}) collective-permute-start(bf16[512,512]{0,1:T(8,128)(2,1)} %slice.16), channel_id=1, source_target_pairs={{0,4},{4,8},{8,12},{12,16},{16,20},{20,24},{24,28},{1,5},{5,9},{9,... | collective-permute-start | bytes 1572872 | tf_op jit(solution)/shard_map/ppermute | solution.py:27
  16.1 3.5 %collective-permute-start.8 = (bf16[512,512]{0,1:T(8,128)(2,1)}, bf16[512,512]{0,1:T(8,128)(2,1)}, u32[]{:S(2)}, u32[]{:S(2)}) collective-permute-start(bf16[512,512]{0,1:T(8,128)(2,1)} %slice.17), channel_id=1, source_target_pairs={{0,4},{4,8},{8,12},{12,16},{16,20},{20,24},{24,28},{1,5},{5,9},{9,... | collective-permute-start | bytes 1572872 | tf_op jit(solution)/shard_map/ppermute | solution.py:27
  23.2 3.7 %fusion.29 = f32[4,128,128]{2,1,0:T(8,128)} fusion(f32[1024,4,128]{0,2,1:T(8,128)} %bitcast.124, bf16[1024,512]{1,0:T(8,128)(2,1)} %param.11), kind=kOutput, calls=%fused_computation.41 | convolution fusion | flops 805306368 | bytes 3407872 | tf_op jit(solution)/shard_map/thd,the->hde/dot_general | solution.py:87
  30.0 9.3 %collective-permute-done = f32[1,4,128]{2,1,0:T(4,128)S(1)} collective-permute-done((f32[1,4,128]{2,1,0:T(4,128)S(1)}, f32[1,4,128]{2,1,0:T(4,128)S(1)}, u32[]{:S(2)}, u32[]{:S(2)}) %collective-permute-start) | collective-permute-done | bytes 2080 | tf_op jit(solution)/shard_map/ppermute | solution.py:17
  39.2 2.5 collective-permute-start.1
  41.7 4.6 %collective-permute-done.1 = f32[1,4,128]{2,1,0:T(4,128)S(1)} collective-permute-done((f32[1,4,128]{2,1,0:T(4,128)S(1)}, f32[1,4,128]{2,1,0:T(4,128)S(1)}, u32[]{:S(2)}, u32[]{:S(2)}) %collective-permute-start.1) | collective-permute-done | bytes 2080 | tf_op jit(solution)/shard_map/ppermute | solution.py:17
  46.4 6.3 %collective-permute-done.2 = f32[1,4,128]{2,1,0:T(4,128)S(1)} collective-permute-done((f32[1,4,128]{2,1,0:T(4,128)S(1)}, f32[1,4,128]{2,1,0:T(4,128)S(1)}, u32[]{:S(2)}, u32[]{:S(2)}) %collective-permute-start.2) | collective-permute-done | bytes 2080 | tf_op jit(solution)/shard_map/ppermute | solution.py:17
  55.0 4.0 %collective-permute-done.3 = f32[1,4,128]{2,1,0:T(4,128)S(1)} collective-permute-done((f32[1,4,128]{2,1,0:T(4,128)S(1)}, f32[1,4,128]{2,1,0:T(4,128)S(1)}, u32[]{:S(2)}, u32[]{:S(2)}) %collective-permute-start.3) | collective-permute-done | bytes 2080 | tf_op jit(solution)/shard_map/ppermute | solution.py:17
  59.0 6.5 %collective-permute-done.4 = f32[1,4,128]{2,1,0:T(4,128)S(1)} collective-permute-done((f32[1,4,128]{2,1,0:T(4,128)S(1)}, f32[1,4,128]{2,1,0:T(4,128)S(1)}, u32[]{:S(2)}, u32[]{:S(2)}) %collective-permute-start.4) | collective-permute-done | bytes 2080 | tf_op jit(solution)/shard_map/ppermute | solution.py:17
  65.5 6.5 %collective-permute-done.5 = f32[1,4,128]{2,1,0:T(4,128)S(1)} collective-permute-done((f32[1,4,128]{2,1,0:T(4,128)S(1)}, f32[1,4,128]{2,1,0:T(4,128)S(1)}, u32[]{:S(2)}, u32[]{:S(2)}) %collective-permute-start.5) | collective-permute-done | bytes 2080 | tf_op jit(solution)/shard_map/ppermute | solution.py:17
  74.1 4.2 %collective-permute-done.6 = f32[1,4,128]{2,1,0:T(4,128)S(1)} collective-permute-done((f32[1,4,128]{2,1,0:T(4,128)S(1)}, f32[1,4,128]{2,1,0:T(4,128)S(1)}, u32[]{:S(2)}, u32[]{:S(2)}) %collective-permute-start.6) | collective-permute-done | bytes 2080 | tf_op jit(solution)/shard_map/ppermute | solution.py:17
  78.3 2.7 fusion.51
  85.3 2.3 pad_maximum_fusion.1
  87.6 2.6 copy.62
  90.2 77.0 %while.14 = (s32[]{:T(128)}, f32[2,512,4,128]{1,0,3,2:T(2,128)}, s32[2]{0:T(128)S(1)}, s32[1024]{0:T(1024)S(1)}, s32[1536]{0:T(1024)S(1)}, /*index=5*/bf16[1024,...) while((s32[]{:T(128)}, f32[2,512,4,128]{1,0,3,2:T(2,128)}, ...), condition=%wide.region_6.7_spmd.clone.clone, body=%wide.region_3.6_spmd.clone.clone.sunk | while | flops 1650986496 | bytes 49885392 | solution.py:72
  92.9 4.1 %fusion.71 = (f32[4,512]{1,0:T(4,128)S(1)}, f32[4,512,1536]{2,1,0:T(8,128)S(1)}) fusion(pred[512,1536]{1,0:T(8,128)(4,1)S(1)} %and_or_fusion.2, bf16[1536,4,128]{2,0,1:T(8,128)(2,1)S(1)} %get-tuple-element.353, bf16[1024,4,128]{0,2,1:T(8,128)(2,1)} %get-tuple-element.352, s32[]{:T(128)S(6)} %select_n.139), kind=kOutput, calls=%fused_computation.4.clone.1 | convolution fusion | flops 814741504 | bytes 15474692 | tf_op jit(solution)/shard_map/while/body/eval_jaxpr/qhd,khd->hqk/dot_general | solution.py:50
  97.0 3.6 %fusion.72 = f32[4,512]{1,0:T(4,128)S(1)} fusion(f32[4,512,1536]{2,1,0:T(8,128)S(1)} %get-tuple-element.319, f32[4,512]{1,0:T(4,128)S(1)} %get-tuple-element.320, pred[512,1536]{1,0:T(8,128)(4,1)S(1)} %and_or_fusion.2), kind=kLoop, calls=%fused_computation.5.clone.1 | loop fusion | flops 12580864 | bytes 13385728 | tf_op jit(solution)/shard_map/while/body/eval_jaxpr/reduce_sum | solution.py:63
  100.7 6.0 %divide_bitcast_fusion.2 = f32[1,512,4,128]{3,1,2,0:T(8,128)} fusion(bf16[1536,4,128]{2,0,1:T(8,128)(2,1)} %get-tuple-element.354, f32[4,512,1536]{2,1,0:T(8,128)S(1)} %get-tuple-element.319, f32[4,512]{1,0:T(4,128)S(1)} %get-tuple-element.320, pred[512,1536]{1,0:T(8,128)(4,1)S(1)} %and_or_fusion.2, f32[512,4]{0,1:T(4,128)S(1)} %bitcast.131), kind=kOutput, calls=%fused_computation.11.clone.1 | convolution fusion | flops 818151424 | bytes 16007168 | tf_op jit(solution)/shard_map/while/body/eval_jaxpr/hqk,khd->qhd/dot_general | solution.py:64
  106.7 2.4 copy.88
  109.1 19.6 %dynamic_update_slice.10 = f32[2,512,4,128]{1,0,3,2:T(2,128)} dynamic-update-slice(f32[2,512,4,128]{1,0,3,2:T(2,128)} %get-tuple-element.335, f32[1,512,4,128]{1,0,3,2:T(1,128)S(1)} %copy.88, s32[]{:T(128)S(6)} %copy.92, s32[]{:T(128)} %constant.139.clone.1..sunk, s32[]{:T(128)} %constant.139.clone.1..sunk, s32[]{:T(128)} %constant.139.clone.1..sunk) | dynamic-update-slice | bytes 2097156 | tf_op jit(solution)/shard_map/while/body/jit(dynamic_update_index_in_dim)/dynamic_update_slice | solution.py:72
  131.4 4.1 %fusion.71 = (f32[4,512]{1,0:T(4,128)S(1)}, f32[4,512,1536]{2,1,0:T(8,128)S(1)}) fusion(pred[512,1536]{1,0:T(8,128)(4,1)S(1)} %and_or_fusion.2, bf16[1536,4,128]{2,0,1:T(8,128)(2,1)S(1)} %get-tuple-element.353, bf16[1024,4,128]{0,2,1:T(8,128)(2,1)} %get-tuple-element.352, s32[]{:T(128)S(6)} %select_n.139), kind=kOutput, calls=%fused_computation.4.clone.1 | convolution fusion | flops 814741504 | bytes 15474692 | tf_op jit(solution)/shard_map/while/body/eval_jaxpr/qhd,khd->hqk/dot_general | solution.py:50
  135.5 3.6 %fusion.72 = f32[4,512]{1,0:T(4,128)S(1)} fusion(f32[4,512,1536]{2,1,0:T(8,128)S(1)} %get-tuple-element.319, f32[4,512]{1,0:T(4,128)S(1)} %get-tuple-element.320, pred[512,1536]{1,0:T(8,128)(4,1)S(1)} %and_or_fusion.2), kind=kLoop, calls=%fused_computation.5.clone.1 | loop fusion | flops 12580864 | bytes 13385728 | tf_op jit(solution)/shard_map/while/body/eval_jaxpr/reduce_sum | solution.py:63
  139.2 6.0 %divide_bitcast_fusion.2 = f32[1,512,4,128]{3,1,2,0:T(8,128)} fusion(bf16[1536,4,128]{2,0,1:T(8,128)(2,1)} %get-tuple-element.354, f32[4,512,1536]{2,1,0:T(8,128)S(1)} %get-tuple-element.319, f32[4,512]{1,0:T(4,128)S(1)} %get-tuple-element.320, pred[512,1536]{1,0:T(8,128)(4,1)S(1)} %and_or_fusion.2, f32[512,4]{0,1:T(4,128)S(1)} %bitcast.131), kind=kOutput, calls=%fused_computation.11.clone.1 | convolution fusion | flops 818151424 | bytes 16007168 | tf_op jit(solution)/shard_map/while/body/eval_jaxpr/hqk,khd->qhd/dot_general | solution.py:64
  145.2 2.4 copy.88
  147.6 19.6 %dynamic_update_slice.10 = f32[2,512,4,128]{1,0,3,2:T(2,128)} dynamic-update-slice(f32[2,512,4,128]{1,0,3,2:T(2,128)} %get-tuple-element.335, f32[1,512,4,128]{1,0,3,2:T(1,128)S(1)} %copy.88, s32[]{:T(128)S(6)} %copy.92, s32[]{:T(128)} %constant.139.clone.1..sunk, s32[]{:T(128)} %constant.139.clone.1..sunk, s32[]{:T(128)} %constant.139.clone.1..sunk) | dynamic-update-slice | bytes 2097156 | tf_op jit(solution)/shard_map/while/body/jit(dynamic_update_index_in_dim)/dynamic_update_slice | solution.py:72
  167.2 4.1 %reshape.244 = f32[1024,4,128]{0,2,1:T(8,128)} reshape(f32[2,512,4,128]{1,0,3,2:T(2,128)} %get-tuple-element.133) | data formatting | bytes 4194304 | tf_op jit(solution)/shard_map/reshape | solution.py:73
  171.3 4.6 %fusion.27 = f32[4,1,128,128]{3,1,2,0:T(1,128)S(1)} fusion(f32[8,4,1,1]{0,2,3,1:T(1,128)S(1)} %bitcast.132, f32[8,4,128,128]{3,2,1,0:T(8,128)} %bitcast.128), kind=kOutput, calls=%fused_computation.36 | convolution fusion | flops 6291456 | bytes 2359424 | tf_op jit(solution)/shard_map/nh,nhde->hde/dot_general | solution.py:101
  175.9 4.8 %fusion.26 = bf16[1024,4,128]{0,2,1:T(8,128)(2,1)} fusion(f32[1024,4,128]{0,2,1:T(8,128)} %reshape.244, f32[4,128,128]{2,1,0:T(8,128)S(1)} %bitcast.130, f32[1024,4,128]{0,2,1:T(8,128)S(1)} %bitcast.123, f32[4]{0:T(128)S(1)} %get-tuple-element.244, f32[1024,4]{0,1:T(4,128)S(1)} %fusion.32, f32[4]{0:T(128)S(1)} %get-tuple-element.245), kind=kOutput, calls=%fused_computation.35 | convolution fusion | flops 807927808 | bytes 5521440 | tf_op jit(solution)/shard_map/thd,hde->the/dot_general | solution.py:114
  180.7 6.6 %copy.64 = bf16[512,4096]{0,1:T(8,128)(2,1)} copy(bf16[512,4096]{1,0:T(8,128)(2,1)} %param.15) | data formatting | bytes 8388608 | tf_op args[6]
  187.3 68.8 %all_to_all.19 = bf16[512,4,1024]{0,2,1:T(8,128)(2,1)} all-to-all(bf16[512,4,1024]{0,2,1:T(8,128)(2,1)} %bitcast.121), channel_id=1, replica_groups=mesh['seq'=8,'head'=4] {'head'}, dimensions={1} | all-to-all | bytes 8388608 | tf_op jit(solution)/shard_map/all_to_all | solution.py:142
  256.0 6.4 %copy.65 = bf16[4,512,1024]{2,1,0:T(8,128)(2,1)} copy(bf16[4,512,1024]{1,2,0:T(8,128)(2,1)} %bitcast.120) | data formatting | bytes 8388608 | tf_op jit(solution)/shard_map/all_to_all | solution.py:142
  262.4 9.4 %convolution_convert_fusion = bf16[1024,1024]{1,0:T(8,128)(2,1)} fusion(bf16[1024,2048]{0,1:T(8,128)(2,1)} %all-gather.4.cloned.1.call-done, bf16[2048,1024]{1,0:T(8,128)(2,1)} %bitcast.127), kind=kOutput, calls=%fused_computation.38 | convolution fusion | flops 4296015872 | bytes 10485760 | tf_op jit(solution)/shard_map/dot_general | solution.py:143
  (70 shorter events, 23.5 us)
Async XLA Ops:
  6.5 21.1 %copy-start = (s32[16,2]{0,1:T(2,128)S(1)}, s32[16,2]{0,1:T(2,128)}, u32[]{:S(2)}) copy-start(s32[16,2]{0,1:T(2,128)} %param.12) | copy-start | bytes 388
  6.5 8.2 %copy-start.5 = (bf16[1024,512]{1,0:T(8,128)(2,1)S(1)}, bf16[1024,512]{1,0:T(8,128)(2,1)}, u32[]{:S(2)}) copy-start(bf16[1024,512]{1,0:T(8,128)(2,1)} %param.11) | copy-start | bytes 3145732
  6.5 164.7 %all-gather.6.cloned.1.call-start = ((), (), s32[]{:S(2)}) async-start(), calls=%async_computation.2 | async-start | bytes 2359296 | tf_op jit(solution)/shard_map/all_gather | solution.py:93
  8.1 8.0 %copy-start.3 = (bf16[1024,512]{0,1:T(8,128)(2,1)}, bf16[1024,512]{0,1:T(8,128)(2,1)S(1)}, u32[]{:S(2)}) copy-start(bf16[1024,512]{0,1:T(8,128)(2,1)S(1)} %copy.56) | copy-start | bytes 3145732
  9.0 72.0 %collective-permute-start.7 = (bf16[512,512]{0,1:T(8,128)(2,1)}, bf16[512,512]{0,1:T(8,128)(2,1)}, u32[]{:S(2)}, u32[]{:S(2)}) collective-permute-start(bf16[512,512]{0,1:T(8,128)(2,1)} %slice.16), channel_id=1, source_target_pairs={{0,4},{4,8},{8,12},{12,16},{16,20},{20,24},{24,28},{1,5},{5,9},{9,... | collective-permute-start | bytes 1572872 | tf_op jit(solution)/shard_map/ppermute | solution.py:27
  16.1 69.2 %collective-permute-start.8 = (bf16[512,512]{0,1:T(8,128)(2,1)}, bf16[512,512]{0,1:T(8,128)(2,1)}, u32[]{:S(2)}, u32[]{:S(2)}) collective-permute-start(bf16[512,512]{0,1:T(8,128)(2,1)} %slice.17), channel_id=1, source_target_pairs={{0,4},{4,8},{8,12},{12,16},{16,20},{20,24},{24,28},{1,5},{5,9},{9,... | collective-permute-start | bytes 1572872 | tf_op jit(solution)/shard_map/ppermute | solution.py:27
  23.2 4.6 %copy-start.6 = (f32[8,4]{0,1:T(4,128)S(1)}, f32[8,4]{0,1:T(4,128)}, u32[]{:S(2)}) copy-start(f32[8,4]{0,1:T(4,128)} %param.13) | copy-start | bytes 388
  26.9 3.0 %copy-start.7 = (f32[4]{0:T(128)S(1)}, f32[4]{0:T(128)}, u32[]{:S(2)}) copy-start(f32[4]{0:T(128)} %param.14) | copy-start | bytes 52
  26.9 235.5 %all-gather.4.cloned.1.call-start = ((), (), s32[]{:S(2)}) async-start(), calls=%async_computation.1 | async-start | bytes 5242880 | tf_op jit(solution)/shard_map/all_gather | solution.py:141
  27.0 12.3 %collective-permute-start = (f32[1,4,128]{2,1,0:T(4,128)S(1)}, f32[1,4,128]{2,1,0:T(4,128)S(1)}, u32[]{:S(2)}, u32[]{:S(2)}) collective-permute-start(f32[1,4,128]{2,1,0:T(4,128)S(1)} %bitcast.134), channel_id=1, source_target_pairs={{0,4},{4,8},{8,12},{12,16},{16,20},{20,24},{24,28},{28,0},{1,5},{5... | collective-permute-start | bytes 6152 | tf_op jit(solution)/shard_map/ppermute | solution.py:17
  39.2 7.1 %collective-permute-start.1 = (f32[1,4,128]{2,1,0:T(4,128)S(1)}, f32[1,4,128]{2,1,0:T(4,128)S(1)}, u32[]{:S(2)}, u32[]{:S(2)}) collective-permute-start(f32[1,4,128]{2,1,0:T(4,128)S(1)} %collective-permute-done), channel_id=1, source_target_pairs={{0,4},{4,8},{8,12},{12,16},{16,20},{20,24},{24,28},{28,0},{1,5},{5... | collective-permute-start | bytes 6152 | tf_op jit(solution)/shard_map/ppermute | solution.py:17
  46.3 6.3 %collective-permute-start.2 = (f32[1,4,128]{2,1,0:T(4,128)S(1)}, f32[1,4,128]{2,1,0:T(4,128)S(1)}, u32[]{:S(2)}, u32[]{:S(2)}) collective-permute-start(f32[1,4,128]{2,1,0:T(4,128)S(1)} %collective-permute-done.1), channel_id=1, source_target_pairs={{0,4},{4,8},{8,12},{12,16},{16,20},{20,24},{24,28},{28,0},{1,5},{5... | collective-permute-start | bytes 6152 | tf_op jit(solution)/shard_map/ppermute | solution.py:17
  52.6 6.4 %collective-permute-start.3 = (f32[1,4,128]{2,1,0:T(4,128)S(1)}, f32[1,4,128]{2,1,0:T(4,128)S(1)}, u32[]{:S(2)}, u32[]{:S(2)}) collective-permute-start(f32[1,4,128]{2,1,0:T(4,128)S(1)} %collective-permute-done.2), channel_id=1, source_target_pairs={{0,4},{4,8},{8,12},{12,16},{16,20},{20,24},{24,28},{28,0},{1,5},{5... | collective-permute-start | bytes 6152 | tf_op jit(solution)/shard_map/ppermute | solution.py:17
  59.0 6.5 %collective-permute-start.4 = (f32[1,4,128]{2,1,0:T(4,128)S(1)}, f32[1,4,128]{2,1,0:T(4,128)S(1)}, u32[]{:S(2)}, u32[]{:S(2)}) collective-permute-start(f32[1,4,128]{2,1,0:T(4,128)S(1)} %collective-permute-done.3), channel_id=1, source_target_pairs={{0,4},{4,8},{8,12},{12,16},{16,20},{20,24},{24,28},{28,0},{1,5},{5... | collective-permute-start | bytes 6152 | tf_op jit(solution)/shard_map/ppermute | solution.py:17
  65.5 6.5 %collective-permute-start.5 = (f32[1,4,128]{2,1,0:T(4,128)S(1)}, f32[1,4,128]{2,1,0:T(4,128)S(1)}, u32[]{:S(2)}, u32[]{:S(2)}) collective-permute-start(f32[1,4,128]{2,1,0:T(4,128)S(1)} %collective-permute-done.4), channel_id=1, source_target_pairs={{0,4},{4,8},{8,12},{12,16},{16,20},{20,24},{24,28},{28,0},{1,5},{5... | collective-permute-start | bytes 6152 | tf_op jit(solution)/shard_map/ppermute | solution.py:17
  72.0 6.3 %collective-permute-start.6 = (f32[1,4,128]{2,1,0:T(4,128)S(1)}, f32[1,4,128]{2,1,0:T(4,128)S(1)}, u32[]{:S(2)}, u32[]{:S(2)}) collective-permute-start(f32[1,4,128]{2,1,0:T(4,128)S(1)} %collective-permute-done.5), channel_id=1, source_target_pairs={{0,4},{4,8},{8,12},{12,16},{16,20},{20,24},{24,28},{28,0},{1,5},{5... | collective-permute-start | bytes 6152 | tf_op jit(solution)/shard_map/ppermute | solution.py:17
  73.8 7.2 %copy-start.4 = (bf16[1024,512]{0,1:T(8,128)(2,1)S(1)}, bf16[1024,512]{0,1:T(8,128)(2,1)}, u32[]{:S(2)}) copy-start(bf16[1024,512]{0,1:T(8,128)(2,1)} %copy-done.3) | copy-start | bytes 3145732
  171.3 4.6 %copy-start.2 = (f32[1024,512]{0,1:T(8,128)S(1)}, f32[1024,512]{0,1:T(8,128)}, u32[]{:S(2)}) copy-start(f32[1024,512]{0,1:T(8,128)} %copy.78) | copy-start | bytes 6291460
  262.4 9.4 %copy-start.1 = (s32[16,2]{0,1:T(2,128)S(1)}, s32[16,2]{0,1:T(2,128)}, u32[]{:S(2)}) copy-start(s32[16,2]{0,1:T(2,128)} %param.12) | copy-start | bytes 388
Sparse Core Ops, SparseCore 0:
  27.0 49.7 all-gather.5
  180.8 46.7 all-gather.3
